TPU v7x, 32 devices: a whole 2x2x4 slice. The times are simulated.
32 devices in a mesh: grp: 2 (over x), seq: 8 (over z, y), kv: 2 (over core).
Axes of the slice: x: 2, y: 2, z: 4, core: 2. Of those that a mesh axis runs over, the one named last changes fastest.
Arguments:
- queries: bfloat16 [4, 64, 128], P(('grp', 'kv'), 'seq'), parts along dimension 0, may hold values from -256 to 256
- keys: bfloat16 [4, 16384, 8, 128], P(('grp', 'kv'), 'seq'), parts along dimension 0, may hold values from -6 to 6
- values: bfloat16 [4, 16384, 8, 128], P(('grp', 'kv'), 'seq'), parts along dimension 0, may hold values from -6 to 6
- picks: int32 [4, 64, 3], P(('grp', 'kv'), 'seq'), parts along dimension 0, may hold values from 0 to 31, as said below
- lengths: int32 [4], P(('grp', 'kv')), parts along dimension 0, may hold values from 8194 to 16384, as said below
Outputs:
- attended: bfloat16 [4, 64, 128], P(('grp', 'kv'), 'seq'), parts along dimension 0
There are 2 independent parts, one for each index of `grp`. A program takes and returns all parts, laid end to end along the dimension named above; each array names one. Nothing has to cross between parts.
Inputs may be any that keep to these rules, and one draw needn't show every extreme that they name: `picks`: each row of 3 holds distinct block numbers in ascending order; the last is the block that holds position lengths[b] - 1, the others lie before it. Position lengths[b] - 1 is never the first position of its block.
All inputs are finite; a program needn't handle non-finite values.
Results may differ from a plain program's by a relative error of at most 0.0046.
Values may be sent and summed in bfloat16 or wider, within the bound.
A program may use at most 64 MiB of HBM per device.

v0:
```python
import math
import jax
import jax.numpy as jnp
from jax import lax
from jax.sharding import PartitionSpec as P

BLOCK = 512
NEGATIVE = -1e30


def shards(queries, keys, values, picks, lengths):
    rows = queries.shape[0]
    head_dim = queries.shape[2]
    local_len = keys.shape[1]
    kv_heads = keys.shape[2]
    blocks_here = local_len // BLOCK
    seq_index = lax.axis_index("seq")
    all_queries, all_picks = (
        lax.all_gather(queries, "seq", axis=1, tiled=True),
        lax.all_gather(picks, "seq", axis=1, tiled=True),
    )
    heads = all_queries.shape[1]
    group = heads // kv_heads
    grouped = all_queries.reshape(rows, kv_heads, group, head_dim)
    scores = jnp.einsum("bkgd,btkd->bkgt", grouped, keys, preferred_element_type=jnp.float32) * (
        1.0 / math.sqrt(head_dim)
    )
    scores = scores.reshape(rows, kv_heads, group, blocks_here, BLOCK)
    block_ids = seq_index * blocks_here + jnp.arange(blocks_here, dtype=jnp.int32)
    chosen = jnp.any(all_picks[:, :, :, None] == block_ids[None, None, None, :], axis=2)
    chosen = chosen.reshape(rows, kv_heads, group, blocks_here)
    positions = block_ids[:, None] * BLOCK + jnp.arange(BLOCK, dtype=jnp.int32)[None, :]
    inside = positions[None, :, :] < lengths[:, None, None]
    live = jnp.logical_and(chosen[..., None], inside[:, None, None, :, :])
    masked = jnp.where(live, scores, -jnp.inf)
    any_live = jnp.any(live, axis=-1)
    safe_max = jnp.where(any_live, jnp.max(masked, axis=-1), NEGATIVE)
    weight = jnp.exp(masked - safe_max[..., None])
    block_total = jnp.sum(weight, axis=-1)
    rounded = weight.astype(jnp.bfloat16)
    blocked_values = values.reshape(rows, blocks_here, BLOCK, kv_heads, head_dim)
    block_out = jnp.einsum(
        "bkgnt,bntkd->bkgnd", rounded, blocked_values, preferred_element_type=jnp.float32
    )
    device_max = jnp.max(safe_max, axis=-1)
    coef = jnp.exp(safe_max - device_max[..., None])
    partial_out = jnp.sum(block_out * coef[..., None], axis=3).reshape(rows, heads, head_dim)
    partial_total = jnp.sum(block_total * coef, axis=-1).reshape(rows, heads)
    partial_max = device_max.reshape(rows, heads)
    came_out, came_max, came_total = (
        lax.all_to_all(partial_out[None], "seq", split_axis=2, concat_axis=0, tiled=True),
        lax.all_to_all(partial_max[None], "seq", split_axis=2, concat_axis=0, tiled=True),
        lax.all_to_all(partial_total[None], "seq", split_axis=2, concat_axis=0, tiled=True),
    )
    top = jnp.max(came_max, axis=0)
    rescale = jnp.exp(came_max - top[None])
    mine_out = jnp.sum(came_out * rescale[..., None], axis=0)
    mine_total = jnp.sum(came_total * rescale, axis=0)
    return (mine_out / mine_total[..., None]).astype(jnp.bfloat16)


def solution(mesh):
    return jax.shard_map(
        shards,
        mesh=mesh,
        in_specs=(
            P(("grp", "kv"), "seq", None),
            P(("grp", "kv"), "seq", None, None),
            P(("grp", "kv"), "seq", None, None),
            P(("grp", "kv"), "seq", None),
            P(("grp", "kv")),
        ),
        out_specs=P(("grp", "kv"), "seq", None),
        check_vma=False,
    )
```

profile of v0, /device:TPU:0, one launch (start us, length us, event | category | flops | bytes accessed | tf_op | source)
XLA Modules:
  0.0 97.5 jit_solution(2691425866918644044)
XLA Ops:
  0.7 0.8 copy.28
  1.4 28.1 %all_gather.7 = bf16[1,64,128]{2,1,0:T(8,128)(2,1)S(1)} all-gather(bf16[1,8,128]{2,1,0:T(8,128)(2,1)} %param.5), channel_id=1, replica_groups=mesh['grp'=2,'seq'=8,'kv'=2] {'seq'}, dimensions={1}, use_global_device_ids=true | all-gather | bytes 18432 | tf_op jit(solution)/shard_map/all_gather | solution.py:19
  29.5 30.6 %all_gather.6 = s32[1,64,3]{2,0,1:T(1,128)S(1)} all-gather(s32[1,8,3]{2,0,1:T(1,128)S(1)} %copy.28), channel_id=1, replica_groups=mesh['grp'=2,'seq'=8,'kv'=2] {'seq'}, dimensions={1}, use_global_device_ids=true | all-gather | bytes 864 | tf_op jit(solution)/shard_map/all_gather | solution.py:20
  60.1 0.1 compare_reduce_fusion
  60.2 0.1 and.40
  60.4 0.7 and_reduce_fusion
  61.1 3.4 %fusion.4 = f32[8,8,2048]{2,1,0:T(8,128)S(1)} fusion(bf16[2048,8,128]{2,1,0:T(8,128)(2,1)} %bitcast.31, bf16[1,64,128]{2,1,0:T(8,128)(2,1)S(1)} %all_gather.7), kind=kOutput, calls=%fused_computation.4 | convolution fusion | flops 33685504 | bytes 4734976 | tf_op jit(solution)/shard_map/bkgd,btkd->bkgt/dot_general | solution.py:25
  64.5 0.2 fusion.16
  64.8 0.7 broadcast_in_dim_reshape.13
  65.5 3.9 %all-to-all-start.1 = ((f32[1,1,64]{1,0,2:T(1,128)}), f32[1,1,64]{1,0,2:T(1,128)S(1)}, u32[]{:S(2)}, u32[]{:S(2)}) async-start(f32[1,1,64]{1,0,2:T(1,128)} %broadcast_in_dim_reshape.13), calls=%async_computation.1 | async-start | bytes 65536 | tf_op jit(solution)/shard_map/all_to_all | solution.py:52
  69.4 0.3 exponential_reduce_fusion
  69.7 0.7 broadcast_in_dim_reshape.14
  70.4 5.6 %all-to-all-done.1 = f32[1,1,64]{1,0,2:T(1,128)S(1)} async-done(((f32[1,1,64]{1,0,2:T(1,128)}), f32[1,1,64]{1,0,2:T(1,128)S(1)}, u32[]{:S(2)}, u32[]{:S(2)}) %all-to-all-start.1) | async-done | bytes 288 | tf_op jit(solution)/shard_map/all_to_all | solution.py:52
  76.1 3.3 %all-to-all-start.2 = ((f32[1,1,64]{1,0,2:T(1,128)}), f32[1,1,64]{1,0,2:T(1,128)S(1)}, u32[]{:S(2)}, u32[]{:S(2)}) async-start(f32[1,1,64]{1,0,2:T(1,128)} %broadcast_in_dim_reshape.14), calls=%async_computation.2 | async-start | bytes 65536 | tf_op jit(solution)/shard_map/all_to_all | solution.py:53
  79.4 4.1 %fusion.13 = f32[8,8,128]{2,1,0:T(8,128)} fusion(bf16[4,512,8,128]{3,2,1,0:T(8,128)(2,1)} %bitcast.34, f32[8,8,4,512]{3,1,2,0:T(8,128)S(1)} %bitcast.30, f32[8,8,4]{1,2,0:T(4,128)S(1)} %get-tuple-element.8, pred[4,512]{1,0:T(4,128)(4,1)S(1)} %add_compare_fusion, pred[8,8,4]{1,2,0:T(4,128)(4,1)S(1)} %copy.30, f32[8,8,4]{1,2,0:T(4,128)S(1)} %get-tuple-element.6), kind=kOutput, calls=%fused_computation.7 | convolution fusion | flops 34136064 | bytes 4755712 | tf_op jit(solution)/shard_map/bkgnt,bntkd->bkgnd/dot_general | solution.py:42
  83.5 0.6 reduce.12
  84.0 0.1 all_to_all.32
  84.1 0.1 all_to_all.35
  84.2 1.9 %all-to-all-done.2 = f32[1,1,64]{1,0,2:T(1,128)S(1)} async-done(((f32[1,1,64]{1,0,2:T(1,128)}), f32[1,1,64]{1,0,2:T(1,128)S(1)}, u32[]{:S(2)}, u32[]{:S(2)}) %all-to-all-start.2) | async-done | bytes 288 | tf_op jit(solution)/shard_map/all_to_all | solution.py:53
  86.0 4.1 %all-to-all-start = ((f32[1,1,64,128]{3,1,0,2:T(1,128)}), f32[1,1,64,128]{3,1,0,2:T(1,128)S(1)}, u32[]{:S(2)}, u32[]{:S(2)}) async-start(f32[1,1,64,128]{3,1,0,2:T(1,128)} %bitcast.10), calls=%async_computation | async-start | bytes 65536 | tf_op jit(solution)/shard_map/all_to_all | solution.py:51
  90.1 0.6 reduce.13
  90.7 0.1 all_to_all.34
  90.8 6.0 %all-to-all-done = f32[1,1,64,128]{3,1,0,2:T(1,128)S(1)} async-done(((f32[1,1,64,128]{3,1,0,2:T(1,128)}), f32[1,1,64,128]{3,1,0,2:T(1,128)S(1)}, u32[]{:S(2)}, u32[]{:S(2)}) %all-to-all-start) | async-done | bytes 32800 | tf_op jit(solution)/shard_map/all_to_all | solution.py:51
  96.9 0.7 fusion.22
  (11 shorter events, 0.3 us)
Async XLA Ops:
  65.5 10.5 %all-to-all-start.1 = ((f32[1,1,64]{1,0,2:T(1,128)}), f32[1,1,64]{1,0,2:T(1,128)S(1)}, u32[]{:S(2)}, u32[]{:S(2)}) async-start(f32[1,1,64]{1,0,2:T(1,128)} %broadcast_in_dim_reshape.13), calls=%async_computation.1 | async-start | bytes 65536 | tf_op jit(solution)/shard_map/all_to_all | solution.py:52
  76.1 10.0 %all-to-all-start.2 = ((f32[1,1,64]{1,0,2:T(1,128)}), f32[1,1,64]{1,0,2:T(1,128)S(1)}, u32[]{:S(2)}, u32[]{:S(2)}) async-start(f32[1,1,64]{1,0,2:T(1,128)} %broadcast_in_dim_reshape.14), calls=%async_computation.2 | async-start | bytes 65536 | tf_op jit(solution)/shard_map/all_to_all | solution.py:53
  86.0 10.8 %all-to-all-start = ((f32[1,1,64,128]{3,1,0,2:T(1,128)}), f32[1,1,64,128]{3,1,0,2:T(1,128)S(1)}, u32[]{:S(2)}, u32[]{:S(2)}) async-start(f32[1,1,64,128]{3,1,0,2:T(1,128)} %bitcast.10), calls=%async_computation | async-start | bytes 65536 | tf_op jit(solution)/shard_map/all_to_all | solution.py:51
where the time goes:
time: 98 us; the launch traced here: 97.5 us
  blocking collectives  58.7 us (60%)
  waiting for transfers between devices  13.5 us (14%)
  starting transfers between devices  11.3 us (12%)
  matrix products  7.44 us (8%)
  other arithmetic  3.38 us (3%)
  local copies, waits for them, and re-layouts  2.59 us (3%)
    all_gather x1, blocking collectives, shards(): lax.all_gather(picks, 'seq', axis=1, tiled=True)  30.6 us
    all_gather x1, blocking collectives, shards(): lax.all_gather(queries, 'seq', axis=1, tiled=True)  28.1 us
    all_to_all x1, waiting for transfers between devices, shards(): lax.all_to_all(partial_out[None], 'seq', split_axis=2, concat_axis=0, til...  5.99 us
    all_to_all x1, waiting for transfers between devices, shards(): lax.all_to_all(partial_max[None], 'seq', split_axis=2, concat_axis=0, til...  5.64 us
    all_to_all x1, starting transfers between devices, shards(): lax.all_to_all(partial_out[None], 'seq', split_axis=2, concat_axis=0, til...  4.09 us
    dot_general x1, matrix products, shards(): jnp.einsum('bkgnt,bntkd->bkgnd', rounded, blocked_values, preferred_eleme...  4.05 us
    all_to_all x1, starting transfers between devices, shards(): lax.all_to_all(partial_max[None], 'seq', split_axis=2, concat_axis=0, til...  3.86 us
    dot_general x1, matrix products, shards(): jnp.einsum('bkgd,btkd->bkgt', grouped, keys, preferred_element_type=jnp.f...  3.38 us
  transfers between devices with their start and end apart: 3, of which 3 were waited for; matrix products, arithmetic and copies ran while one was open for 6% of the time, Pallas kernels for 0%

commit v1 on v0

--- a/solution.py
+++ b/solution.py
@@ -3,9 +3,22 @@
 import jax.numpy as jnp
 from jax import lax
 from jax.sharding import PartitionSpec as P
+from jax.lax import all_to_all, axis_size
 
 BLOCK = 512
 NEGATIVE = -1e30
+
+
+def try_all_ends(field_in, which_axis):
+    return jnp.concatenate(
+        all_to_all(
+            jnp.stack(jnp.split(field_in, axis_size(which_axis), 2), axis=0),
+            axis_name=which_axis,
+            split_axis=0,
+            concat_axis=0,
+        ),
+        0,
+    )
 
 
 def shards(queries, keys, values, picks, lengths):
@@ -49,7 +62,7 @@
     partial_max = device_max.reshape(rows, heads)
     came_out, came_max, came_total = (
         lax.all_to_all(partial_out[None], "seq", split_axis=2, concat_axis=0, tiled=True),
-        lax.all_to_all(partial_max[None], "seq", split_axis=2, concat_axis=0, tiled=True),
+        try_all_ends(partial_max[None], which_axis="seq"),
         lax.all_to_all(partial_total[None], "seq", split_axis=2, concat_axis=0, tiled=True),
     )
     top = jnp.max(came_max, axis=0)

time: 98 us -> 99.2 us (1.012)
  local copies, waits for them, and re-layouts: 2.59 us -> 6.65 us
  waiting for transfers between devices: 13.5 us -> 10.2 us
  starting transfers between devices: 11.3 us -> 12.3 us
    unnamed x1 -> x8, local copies, waits for them, and re-layouts: 0.76 us -> 4.95 us
    all_to_all x1, waiting for transfers between devices: 5.64 us -> 1.8 us  [try_all_ends(): all_to_all(jnp.stack(jnp.split(field_in, axis_size(which_axis), 2), axis=...]
  transfers between devices with their start and end apart: 3 -> 3, of which waited for: 3 -> 3; matrix products, arithmetic and copies ran while one was open for 6% -> 10% of each run, Pallas kernels for 0% -> 0%
where the time goes in v1:
time: 99.2 us; the launch traced here: 98.8 us
  blocking collectives  58.7 us (59%)
  starting transfers between devices  12.3 us (12%)
  waiting for transfers between devices  10.2 us (10%)
  matrix products  7.43 us (7%)
  local copies, waits for them, and re-layouts  6.65 us (7%)
  other arithmetic  2.84 us (3%)
    all_gather x1, blocking collectives, shards(): lax.all_gather(picks, 'seq', axis=1, tiled=True)  30.6 us
    all_gather x1, blocking collectives, shards(): lax.all_gather(queries, 'seq', axis=1, tiled=True)  28.1 us
    all_to_all x1, waiting for transfers between devices, shards(): lax.all_to_all(partial_out[None], 'seq', split_axis=2, concat_axis=0, til...  6.63 us
    unnamed x8, local copies, waits for them, and re-layouts  4.95 us
    all_to_all x1, starting transfers between devices, try_all_ends(): all_to_all(jnp.stack(jnp.split(field_in, axis_size(which_axis), 2), axis=...  4.24 us
    all_to_all x1, starting transfers between devices, shards(): lax.all_to_all(partial_out[None], 'seq', split_axis=2, concat_axis=0, til...  4.2 us
    dot_general x1, matrix products, shards(): jnp.einsum('bkgnt,bntkd->bkgnd', rounded, blocked_values, preferred_eleme...  4.05 us
    all_to_all x1, starting transfers between devices, shards(): lax.all_to_all(partial_total[None], 'seq', split_axis=2, concat_axis=0, t...  3.86 us
  transfers between devices with their start and end apart: 3, of which 3 were waited for; matrix products, arithmetic and copies ran while one was open for 10% of the time, Pallas kernels for 0%

profile of v1, /device:TPU:0, one launch (start us, length us, event | category | flops | bytes accessed | tf_op | source)
XLA Modules:
  0.0 98.8 jit_solution(16684929771123456427)
XLA Ops:
  0.0 28.1 %all_gather.7 = bf16[1,64,128]{2,1,0:T(8,128)(2,1)S(1)} all-gather(bf16[1,8,128]{2,1,0:T(8,128)(2,1)} %param.5), channel_id=1, replica_groups=mesh['grp'=2,'seq'=8,'kv'=2] {'seq'}, dimensions={1}, use_global_device_ids=true | all-gather | bytes 18432 | tf_op jit(solution)/shard_map/all_gather | solution.py:32
  28.7 0.8 copy.26
  29.5 30.6 %all_gather.6 = s32[1,64,3]{2,0,1:T(1,128)S(1)} all-gather(s32[1,8,3]{2,0,1:T(1,128)S(1)} %copy.26), channel_id=1, replica_groups=mesh['grp'=2,'seq'=8,'kv'=2] {'seq'}, dimensions={1}, use_global_device_ids=true | all-gather | bytes 864 | tf_op jit(solution)/shard_map/all_gather | solution.py:33
  60.4 3.4 %fusion.4 = f32[8,8,2048]{2,1,0:T(8,128)S(1)} fusion(bf16[2048,8,128]{2,1,0:T(8,128)(2,1)} %bitcast.49, bf16[1,64,128]{2,1,0:T(8,128)(2,1)S(1)} %all_gather.7), kind=kOutput, calls=%fused_computation.4 | convolution fusion | flops 33685504 | bytes 4734976 | tf_op jit(solution)/shard_map/bkgd,btkd->bkgt/dot_general | solution.py:38
  63.8 0.7 and_reduce_fusion
  64.8 0.3 exponential_reduce_fusion
  65.2 0.7 broadcast_in_dim_reshape.13
  65.9 3.9 %all-to-all-start.2 = ((f32[1,1,64]{1,0,2:T(1,128)}), f32[1,1,64]{1,0,2:T(1,128)S(1)}, u32[]{:S(2)}, u32[]{:S(2)}) async-start(f32[1,1,64]{1,0,2:T(1,128)} %broadcast_in_dim_reshape.13), calls=%async_computation.2 | async-start | bytes 65536 | tf_op jit(solution)/shard_map/all_to_all | solution.py:66
  69.8 0.5 constant_dynamic-update-slice_fusion.7
  70.3 0.6 constant_dynamic-update-slice_fusion.6
  71.0 0.6 constant_dynamic-update-slice_fusion.5
  71.6 0.6 constant_dynamic-update-slice_fusion.4
  72.2 0.6 constant_dynamic-update-slice_fusion.3
  72.8 0.6 constant_dynamic-update-slice_fusion.2
  73.4 0.6 constant_dynamic-update-slice_fusion.1
  74.0 0.7 constant_dynamic-update-slice_fusion
  74.7 1.8 %all-to-all-done.2 = f32[1,1,64]{1,0,2:T(1,128)S(1)} async-done(((f32[1,1,64]{1,0,2:T(1,128)}), f32[1,1,64]{1,0,2:T(1,128)S(1)}, u32[]{:S(2)}, u32[]{:S(2)}) %all-to-all-start.2) | async-done | bytes 288 | tf_op jit(solution)/shard_map/all_to_all | solution.py:66
  76.4 4.2 %all-to-all-start.1 = ((f32[8,1,1,8]{3,2,1,0:T(1,128)}), f32[8,1,1,8]{3,2,1,0:T(1,128)S(1)}, u32[]{:S(2)}, u32[]{:S(2)}) async-start(f32[8,1,1,8]{3,2,1,0:T(1,128)} %constant_dynamic-update-slice_fusion), calls=%async_computation.1 | async-start | bytes 8192 | tf_op jit(solution)/shard_map/all_to_all | solution.py:14
  80.7 4.0 %fusion.13 = f32[8,8,128]{2,1,0:T(8,128)} fusion(bf16[4,512,8,128]{3,2,1,0:T(8,128)(2,1)} %bitcast.54, f32[8,8,4,512]{3,1,2,0:T(8,128)S(1)} %bitcast.48, f32[8,8,4]{1,2,0:T(4,128)S(1)} %get-tuple-element.8, pred[4,512]{1,0:T(4,128)(4,1)S(1)} %add_compare_fusion, pred[8,8,4]{1,2,0:T(4,128)(4,1)S(1)} %copy.28, f32[8,8,4]{1,2,0:T(4,128)S(1)} %get-tuple-element.6), kind=kOutput, calls=%fused_computation.7 | convolution fusion | flops 34136064 | bytes 4755712 | tf_op jit(solution)/shard_map/bkgnt,bntkd->bkgnd/dot_general | solution.py:55
  84.7 0.6 reduce.13
  85.3 1.8 %all-to-all-done.1 = f32[8,1,1,8]{3,2,1,0:T(1,128)S(1)} async-done(((f32[8,1,1,8]{3,2,1,0:T(1,128)}), f32[8,1,1,8]{3,2,1,0:T(1,128)S(1)}, u32[]{:S(2)}, u32[]{:S(2)}) %all-to-all-start.1) | async-done | bytes 288 | tf_op jit(solution)/shard_map/all_to_all | solution.py:14
  87.1 4.2 %all-to-all-start = ((f32[1,1,64,128]{3,1,0,2:T(1,128)}), f32[1,1,64,128]{3,1,0,2:T(1,128)S(1)}, u32[]{:S(2)}, u32[]{:S(2)}) async-start(f32[1,1,64,128]{3,1,0,2:T(1,128)} %bitcast.10), calls=%async_computation | async-start | bytes 65536 | tf_op jit(solution)/shard_map/all_to_all | solution.py:64
  91.4 6.6 %all-to-all-done = f32[1,1,64,128]{3,1,0,2:T(1,128)S(1)} async-done(((f32[1,1,64,128]{3,1,0,2:T(1,128)}), f32[1,1,64,128]{3,1,0,2:T(1,128)S(1)}, u32[]{:S(2)}, u32[]{:S(2)}) %all-to-all-start) | async-done | bytes 32800 | tf_op jit(solution)/shard_map/all_to_all | solution.py:64
  98.1 0.7 fusion.22
  (16 shorter events, 0.9 us)
Async XLA Ops:
  65.9 10.5 %all-to-all-start.2 = ((f32[1,1,64]{1,0,2:T(1,128)}), f32[1,1,64]{1,0,2:T(1,128)S(1)}, u32[]{:S(2)}, u32[]{:S(2)}) async-start(f32[1,1,64]{1,0,2:T(1,128)} %broadcast_in_dim_reshape.13), calls=%async_computation.2 | async-start | bytes 65536 | tf_op jit(solution)/shard_map/all_to_all | solution.py:66
  76.4 10.7 %all-to-all-start.1 = ((f32[8,1,1,8]{3,2,1,0:T(1,128)}), f32[8,1,1,8]{3,2,1,0:T(1,128)S(1)}, u32[]{:S(2)}, u32[]{:S(2)}) async-start(f32[8,1,1,8]{3,2,1,0:T(1,128)} %constant_dynamic-update-slice_fusion), calls=%async_computation.1 | async-start | bytes 8192 | tf_op jit(solution)/shard_map/all_to_all | solution.py:14
  87.1 10.9 %all-to-all-start = ((f32[1,1,64,128]{3,1,0,2:T(1,128)}), f32[1,1,64,128]{3,1,0,2:T(1,128)S(1)}, u32[]{:S(2)}, u32[]{:S(2)}) async-start(f32[1,1,64,128]{3,1,0,2:T(1,128)} %bitcast.10), calls=%async_computation | async-start | bytes 65536 | tf_op jit(solution)/shard_map/all_to_all | solution.py:64
